TPU v7x, 32 devices: a whole 2x2x4 slice. The times are simulated.
32 devices in a mesh: groups: 2 (over y), section: 4 (over z), tp: 2 (over core), sp: 2 (over x).
Axes of the slice: x: 2, y: 2, z: 4, core: 2. Of those that a mesh axis runs over, the one named last changes fastest.
Arguments:
- hidden: bfloat16 [1024, 6144], P(('groups', 'sp', 'section'), 'tp'), parts along dimension 0, may hold values from -6 to 6
- modulation: float32 [2, 6144], P(None, 'tp'), may hold values from -2 to 2
- time_embed: float32 [12288], P(('groups', 'tp')), parts along dimension 0, may hold values from -2 to 2
- head_weight: bfloat16 [6144, 64], P('tp'), may hold values from -0.078125 to 0.078125
- head_bias: float32 [64], replicated, may hold values from -2 to 2
- noisy: bfloat16 [16, 16, 16, 16], P(('groups', 'sp'), None, 'section'), parts along dimension 0, may hold values from -6 to 6
- step_size: float32 [2], P('groups'), parts along dimension 0, may hold values from 0.2 to 0.6
- latent_mean: float32 [16], replicated, may hold values from -2 to 2
- latent_std: float32 [16], replicated, may hold values from 0.5 to 2
- in_weight: bfloat16 [27, 16, 512], P(None, None, 'tp'), may hold values from -0.3125 to 0.3125
- in_bias: float32 [512], P('tp'), may hold values from -2 to 2
- norm_gain: float32 [512], replicated, may hold values from 0.25 to 1.75
- conv_weight: bfloat16 [27, 512, 512], P(None, 'section', 'tp'), may hold values from -0.0546875 to 0.0546875
- conv_bias: float32 [512], P('tp'), may hold values from -2 to 2
Outputs:
- decoded: bfloat16 [16, 16, 16, 512], P(('groups', 'sp'), None, 'section', 'tp'), parts along dimension 0
There are 2 independent parts, one for each index of `groups`. A program takes and returns all parts, laid end to end along the dimension named above; an argument that names none is the same for every part. Nothing has to cross between parts.
All inputs are finite; a program needn't handle non-finite values.
Results may differ from a plain program's by a relative error of at most 0.006.
Values may be sent and summed in bfloat16 or wider, within the bound.
A program may use at most 128 MiB of HBM per device.

v0:
```python
import jax
import jax.numpy as jnp
from jax import lax
from jax.sharding import PartitionSpec as P

D = 6144


def padded_2(value, sides, width):
    for axis, dim in sides:
        count, length = (lax.axis_size(axis), value.shape[dim])
        up = [(i, (i + 1) % count) for i in range(count - 1)]
        down = [(j, i) for i, j in up]
        last = lax.slice_in_dim(value, length - width, length, axis=dim)
        leading = lax.slice_in_dim(value, 0, width, axis=dim)
        before = lax.ppermute(last, axis, up)
        after = lax.ppermute(leading, axis, down)
        value = jnp.concatenate([before, value, after], axis=dim)
    return value


def passed_along(value, axis, by):
    count = lax.axis_size(axis)
    pairs = [(i, i + by) for i in range(count) if 0 <= i + by < count]
    return lax.ppermute(value, axis, pairs)


def conv_taps(padded, weight, frames, height, columns):
    channels = padded.shape[3]
    result = jnp.zeros((frames * height * columns, weight.shape[2]), jnp.float32)
    for offset_time in range(3):
        for offset_row in range(3):
            slab = padded[offset_time : offset_time + frames, offset_row : offset_row + height]
            window = jnp.concatenate(
                [slab[:, :, 0:columns], slab[:, :, 1 : columns + 1], slab[:, :, 2 : columns + 2]],
                axis=3,
            )
            first = 9 * offset_time + 3 * offset_row
            taps = weight[first : first + 3].reshape(3 * channels, weight.shape[2])
            result = result + jnp.dot(
                window.reshape(-1, 3 * channels), taps, preferred_element_type=jnp.float32
            )
    return result


def activate(source, gain_vector):
    values = source.astype(jnp.float32)
    squares = jnp.mean(values * values, axis=-1, keepdims=True)
    return jax.nn.silu(values * lax.rsqrt(squares + 1e-06) * gain_vector).astype(jnp.bfloat16)


def pad_rows(source):
    return jnp.pad(source, ((0, 0), (1, 1), (0, 0), (0, 0)))


def shards(
    hidden,
    modulation,
    time_embed,
    head_weight,
    head_bias,
    noisy,
    step_size,
    latent_mean,
    latent_std,
    in_weight,
    in_bias,
    norm_gain,
    conv_weight,
    conv_bias,
):
    frames, height, columns, lat_channels = noisy.shape
    sections = lax.axis_size("section")
    half_channels = in_weight.shape[2]
    values = hidden.astype(jnp.float32)
    row_sums, square_sums = lax.psum(
        (jnp.sum(values, axis=1), jnp.sum(values * values, axis=1)), "tp"
    )
    average = row_sums / D
    variance = square_sums / D - average * average
    shift_term = modulation[0] + time_embed
    scale_term = modulation[1] + time_embed
    modulated = (
        (values - average[:, None]) * lax.rsqrt(variance[:, None] + 1e-06) * (1.0 + scale_term)
        + shift_term
    ).astype(jnp.bfloat16)
    partial_sum = jnp.dot(modulated, head_weight, preferred_element_type=jnp.float32)
    velocity = (lax.psum(partial_sum, "tp") + head_bias).astype(jnp.bfloat16)
    band_rows = velocity.shape[0] * 2 // (columns * sections)
    outgoing = velocity.reshape(band_rows, sections, -1)
    arrived = lax.all_to_all(outgoing, "section", split_axis=1, concat_axis=0, tiled=True)
    latent_field = arrived.reshape(frames, height // 2, columns // 2, 2, 2, lat_channels)
    latent_field = jnp.transpose(latent_field, (0, 1, 3, 2, 4, 5)).reshape(
        frames, height, columns, lat_channels
    )
    latent = (
        (noisy.astype(jnp.float32) - step_size[0] * latent_field.astype(jnp.float32)) * latent_std
        + latent_mean
    ).astype(jnp.bfloat16)
    latent_wide = padded_2(latent, (("section", 2),), 2)
    earlier = passed_along(latent_wide, "sp", 1)
    stacked = pad_rows(jnp.concatenate([earlier, latent_wide], axis=0))
    extended = (conv_taps(stacked, in_weight, frames + 2, height, columns + 2) + in_bias).astype(
        jnp.bfloat16
    )
    extended = extended.reshape(frames + 2, height, columns + 2, half_channels)
    upblock_half = extended[2:, :, 1 : columns + 1]
    extended_full = lax.all_gather(extended, "tp", axis=3, tiled=True)
    normed = activate(extended_full, norm_gain)
    frame_index = lax.axis_index("sp") * frames - 2 + jnp.arange(frames + 2, dtype=jnp.int32)
    column_index = (
        lax.axis_index("section") * columns - 1 + jnp.arange(columns + 2, dtype=jnp.int32)
    )
    inside_cols = (column_index >= 0) & (column_index < columns * sections)
    inside = (frame_index >= 0)[:, None, None, None] & inside_cols[None, None, :, None]
    conv_input = pad_rows(jnp.where(inside, normed, jnp.zeros_like(normed)))
    full_weight = lax.all_gather(conv_weight, "section", axis=1, tiled=True)
    mixed = conv_taps(conv_input, full_weight, frames, height, columns)
    decoded = (
        upblock_half.astype(jnp.float32).reshape(-1, half_channels) + mixed + conv_bias
    ).astype(jnp.bfloat16)
    return decoded.reshape(frames, height, columns, half_channels)


def solution(mesh):
    placed = (
        P(("groups", "sp", "section"), "tp"),
        P(None, "tp"),
        P(("groups", "tp")),
        P("tp", None),
        P(),
        P(("groups", "sp"), None, "section", None),
        P("groups"),
        P(),
        P(),
        P(None, None, "tp"),
        P("tp"),
        P(),
        P(None, "section", "tp"),
        P("tp"),
    )
    return jax.shard_map(
        shards,
        mesh=mesh,
        in_specs=placed,
        out_specs=P(("groups", "sp"), None, "section", "tp"),
        check_vma=False,
    )
```

profile of v0, /device:TPU:0, one launch (start us, length us, event | category | flops | bytes accessed | tf_op | source)
XLA Modules:
  0.0 158.0 jit_solution(14631500808163563009)
XLA Ops:
  7.8 2.6 %all-reduce.2 = (f32[64]{0:T(128)S(1)}, f32[64]{0:T(128)S(1)}) all-reduce(f32[64]{0:T(128)S(1)} %get-tuple-element.6, f32[64]{0:T(128)S(1)} %get-tuple-element.5), channel_id=1, replica_groups=mesh['groups'=2,'section'=4,'tp'=2,'sp'=2] {'tp'}, use_global_device_ids=true, to_apply=%region_3.0 | all-reduce | flops 128 | bytes 1024 | tf_op jit(solution)/shard_map/psum | solution.py:76
  10.8 3.6 %psum.23 = f32[64,64]{1,0:T(8,128)S(1)} all-reduce(f32[64,64]{1,0:T(8,128)S(1)} %fusion.19), channel_id=1, replica_groups=mesh['groups'=2,'section'=4,'tp'=2,'sp'=2] {'tp'}, use_global_device_ids=true, to_apply=%region_4.0 | all-reduce | flops 4096 | bytes 32768 | tf_op jit(solution)/shard_map/psum | solution.py:88
  15.1 6.0 %all-to-all-start = ((bf16[8,4,128]{2,0,1:T(8,128)(2,1)}), bf16[8,4,128]{2,0,1:T(8,128)(2,1)S(1)}, u32[]{:S(2)}, u32[]{:S(2)}) async-start(bf16[8,4,128]{2,0,1:T(8,128)(2,1)} %copy.17), calls=%async_computation | async-start | bytes 16384 | tf_op jit(solution)/shard_map/all_to_all | solution.py:91
  22.5 7.5 %all-to-all-done = bf16[8,4,128]{2,0,1:T(8,128)(2,1)S(1)} async-done(((bf16[8,4,128]{2,0,1:T(8,128)(2,1)}), bf16[8,4,128]{2,0,1:T(8,128)(2,1)S(1)}, u32[]{:S(2)}, u32[]{:S(2)}) %all-to-all-start) | async-done | bytes 8224 | tf_op jit(solution)/shard_map/all_to_all | solution.py:91
  30.4 1.3 collective-permute-start
  31.7 1.3 collective-permute-start.1
  33.9 4.4 %collective-permute-done.1 = bf16[4,16,2,16]{3,2,1,0:T(2,128)(2,1)S(1)} collective-permute-done((bf16[4,16,2,16]{3,2,1,0:T(2,128)(2,1)S(1)}, bf16[4,16,2,16]{3,2,1,0:T(2,128)(2,1)S(1)}, u32[]{:S(2)}, u32[]{:S(2)}) %collective-permute-start.1) | collective-permute-done | bytes 4128 | tf_op jit(solution)/shard_map/ppermute | solution.py:17
  38.5 3.4 %collective-permute-start.2 = (bf16[4,16,8,16]{3,2,1,0:T(8,128)(2,1)S(1)}, bf16[4,16,8,16]{3,2,1,0:T(8,128)(2,1)S(1)}, u32[]{:S(2)}, u32[]{:S(2)}) collective-permute-start(bf16[4,16,8,16]{3,2,1,0:T(8,128)(2,1)S(1)} %pad_maximum_fusion.18), channel_id=1, source_target_pairs={{0,1},{2,3},{4,5},{6,7},{8,9},{10,11},{12,13},{14,15},{16,17},{18,... | collective-permute-start | bytes 49160 | tf_op jit(solution)/shard_map/ppermute | solution.py:25
  42.5 1.9 %collective-permute-done.2 = bf16[4,16,8,16]{3,2,1,0:T(8,128)(2,1)S(1)} collective-permute-done((bf16[4,16,8,16]{3,2,1,0:T(8,128)(2,1)S(1)}, bf16[4,16,8,16]{3,2,1,0:T(8,128)(2,1)S(1)}, u32[]{:S(2)}, u32[]{:S(2)}) %collective-permute-start.2) | collective-permute-done | bytes 16416 | tf_op jit(solution)/shard_map/ppermute | solution.py:25
  44.8 1.0 pad_slice_fusion.2
  47.1 1.3 pad_slice_fusion.1
  48.3 1.1 pad_maximum_fusion.10
  50.2 2.2 %pad_maximum_fusion.12 = (bf16[6,16,6,48]{3,2,1,0:T(8,128)(2,1)}, bf16[6,16,6,48]{3,2,1,0:T(8,128)(2,1)S(1)}) fusion(bf16[6,16,6,16]{3,2,1,0:T(8,128)(2,1)S(1)} %get-tuple-element.53, bf16[6,16,6,16]{3,2,1,0:T(8,128)(2,1)S(1)} %get-tuple-element.52, bf16[6,16,6,16]{3,2,1,0:T(8,128)(2,1)S(1)} %get-tuple-element.51, ...), kind=kLoop, calls=%fused_computation.58 | loop fusion | flops 331776 | bytes 221184 | tf_op jit(solution)/shard_map/concatenate | solution.py:34
  52.4 1.7 %reshape.204 = bf16[576,48]{1,0:T(8,128)(2,1)} reshape(bf16[6,16,6,48]{3,2,1,0:T(8,128)(2,1)} %get-tuple-element.91) | data formatting | bytes 110592 | tf_op jit(solution)/shard_map/reshape | solution.py:41
  59.0 2.5 %all_gather.6 = bf16[6,16,6,512]{3,2,1,0:T(8,128)(2,1)S(1)} all-gather(bf16[6,16,6,256]{3,2,1,0:T(8,128)(2,1)S(1)} %reshape.216), channel_id=1, replica_groups=mesh['groups'=2,'section'=4,'tp'=2,'sp'=2] {'tp'}, dimensions={3}, use_global_device_ids=true | all-gather | bytes 884736 | tf_op jit(solution)/shard_map/all_gather | solution.py:108
  62.4 1.4 fusion.26
  64.3 2.3 %pad_slice_fusion.20 = (bf16[4,16,4,512]{3,2,1,0:T(4,128)(2,1)}, bf16[4,16,4,512]{3,2,1,0:T(4,128)(2,1)S(1)}, bf16[4,16,4,512]{3,2,1,0:T(4,128)(2,1)S(1)}, bf16[...) fusion(bf16[6,16,6,512]{3,2,1,0:T(8,128)(2,1)S(1)} %fusion.18), kind=kLoop, calls=%fused_computation.96 | loop fusion | bytes 3670016 | tf_op jit(solution)/shard_map/slice | solution.py:35
  67.2 1.5 pad_maximum_fusion.2
  68.6 1.1 reshape.223
  69.8 1.5 pad_maximum_fusion.3
  71.2 1.1 reshape.225
  72.4 2.5 %pad_slice_fusion.19 = (bf16[4,16,4,512]{3,2,1,0:T(4,128)(2,1)S(1)}, bf16[4,16,4,512]{3,2,1,0:T(4,128)(2,1)}, bf16[4,16,4,512]{3,2,1,0:T(4,128)(2,1)}, bf16[4,16...) fusion(bf16[6,16,6,512]{3,2,1,0:T(8,128)(2,1)S(1)} %fusion.18), kind=kLoop, calls=%fused_computation.95 | loop fusion | bytes 4456448 | tf_op jit(solution)/shard_map/slice | solution.py:35
  75.4 1.5 pad_maximum_fusion.4
  76.8 1.1 reshape.227
  77.9 1.5 pad_maximum_fusion.7
  79.4 1.1 reshape.233
  80.4 1.4 pad_maximum_fusion.5
  81.9 1.1 reshape.229
  82.9 1.4 pad_maximum_fusion.6
  84.4 1.1 reshape.231
  85.5 55.2 %all-gather.2.cloned.1.call-done = bf16[27,512,256]{2,1,0:T(8,128)(2,1)} async-done(((bf16[27,128,256]{2,1,0:T(8,128)(2,1)}), bf16[27,512,256]{2,1,0:T(8,128)(2,1)}) %all-gather.2.cloned.1.call-update) | async-done | bytes 7077904 | tf_op jit(solution)/shard_map/all_gather | solution.py:117
  140.7 3.8 %fusion.25 = (bf16[3,512,256]{2,1,0:T(8,128)(2,1)S(1)}, bf16[3,512,256]{2,1,0:T(8,128)(2,1)S(1)}, bf16[3,512,256]{2,1,0:T(8,128)(2,1)S(1)}, bf16[3,512,256]{2,1,...) fusion(bf16[27,512,256]{2,1,0:T(8,128)(2,1)} %all-gather.2.clon, ...), kind=kLoop, calls=%fused_computation.112 | loop fusion | bytes 14155776 | tf_op jit(solution)/shard_map/slice | solution.py:39
  (142 shorter events, 21.1 us)
Async XLA Ops:
  6.5 3.9 %copy-start = (bf16[3072,64]{0,1:T(8,128)(2,1)S(1)}, bf16[3072,64]{0,1:T(8,128)(2,1)}, u32[]{:S(2)}) copy-start(bf16[3072,64]{0,1:T(8,128)(2,1)} %param.17) | copy-start | bytes 1179652
  6.5 1.1 copy-start.18
  6.5 3.9 %copy-start.31 = (f32[3072]{0:T(1024)S(1)}, f32[3072]{0:T(1024)}, u32[]{:S(2)}) copy-start(f32[3072]{0:T(1024)} %param.16) | copy-start | bytes 36868
  6.5 7.9 %copy-start.36 = (f32[64]{0:T(128)S(1)}, f32[64]{0:T(128)}, u32[]{:S(2)}) copy-start(f32[64]{0:T(128)} %param.18) | copy-start | bytes 772
  6.5 14.6 %copy-start.19 = (bf16[27,16,256]{2,1,0:T(8,128)(2,1)S(1)}, bf16[27,16,256]{2,1,0:T(8,128)(2,1)}, u32[]{:S(2)}) copy-start(bf16[27,16,256]{2,1,0:T(8,128)(2,1)} %param.23) | copy-start | bytes 663556
  6.6 134.1 %all-gather.2.cloned.1.call-start = ((), (), s32[]{:S(2)}) async-start(), calls=%async_computation.1 | async-start | bytes 8847360 | tf_op jit(solution)/shard_map/all_gather | solution.py:117
  7.3 22.9 %copy-start.29 = (bf16[4,16,4,16]{3,2,1,0:T(4,128)(2,1)S(1)}, bf16[4,16,4,16]{3,2,1,0:T(4,128)(2,1)}, u32[]{:S(2)}) copy-start(bf16[4,16,4,16]{3,2,1,0:T(4,128)(2,1)} %param.19) | copy-start | bytes 24580
  7.3 22.9 %copy-start.37 = (f32[16]{0:T(128)S(1)}, f32[16]{0:T(128)}, u32[]{:S(2)}) copy-start(f32[16]{0:T(128)} %param.21) | copy-start | bytes 196
  7.3 23.0 %copy-start.38 = (f32[16]{0:T(128)S(1)}, f32[16]{0:T(128)}, u32[]{:S(2)}) copy-start(f32[16]{0:T(128)} %param.22) | copy-start | bytes 196
  15.1 14.9 %all-to-all-start = ((bf16[8,4,128]{2,0,1:T(8,128)(2,1)}), bf16[8,4,128]{2,0,1:T(8,128)(2,1)S(1)}, u32[]{:S(2)}, u32[]{:S(2)}) async-start(bf16[8,4,128]{2,0,1:T(8,128)(2,1)} %copy.17), calls=%async_computation | async-start | bytes 16384 | tf_op jit(solution)/shard_map/all_to_all | solution.py:91
  30.4 3.5 %collective-permute-start = (bf16[4,16,2,16]{3,2,1,0:T(2,128)(2,1)S(1)}, bf16[4,16,2,16]{3,2,1,0:T(2,128)(2,1)S(1)}, u32[]{:S(2)}, u32[]{:S(2)}) collective-permute-start(bf16[4,16,2,16]{3,2,1,0:T(2,128)(2,1)S(1)} %get-tuple-element.81), channel_id=1, source_target_pairs={{0,4},{4,8},{8,12},{1,5},{5,9},{9,13},{2,6},{6,10},{10,14},{3,7},{... | collective-permute-start | bytes 12296 | tf_op jit(solution)/shard_map/ppermute | solution.py:16
  31.7 6.6 %collective-permute-start.1 = (bf16[4,16,2,16]{3,2,1,0:T(2,128)(2,1)S(1)}, bf16[4,16,2,16]{3,2,1,0:T(2,128)(2,1)S(1)}, u32[]{:S(2)}, u32[]{:S(2)}) collective-permute-start(bf16[4,16,2,16]{3,2,1,0:T(2,128)(2,1)S(1)} %get-tuple-element.82), channel_id=1, source_target_pairs={{4,0},{8,4},{12,8},{5,1},{9,5},{13,9},{6,2},{10,6},{14,10},{7,3},{... | collective-permute-start | bytes 12296 | tf_op jit(solution)/shard_map/ppermute | solution.py:17
  38.5 5.9 %collective-permute-start.2 = (bf16[4,16,8,16]{3,2,1,0:T(8,128)(2,1)S(1)}, bf16[4,16,8,16]{3,2,1,0:T(8,128)(2,1)S(1)}, u32[]{:S(2)}, u32[]{:S(2)}) collective-permute-start(bf16[4,16,8,16]{3,2,1,0:T(8,128)(2,1)S(1)} %pad_maximum_fusion.18), channel_id=1, source_target_pairs={{0,1},{2,3},{4,5},{6,7},{8,9},{10,11},{12,13},{14,15},{16,17},{18,... | collective-permute-start | bytes 49160 | tf_op jit(solution)/shard_map/ppermute | solution.py:25
  49.4 4.6 %copy-start.11 = (bf16[6,16,6,16]{3,2,1,0:T(8,128)(2,1)S(1)}, bf16[6,16,6,16]{3,2,1,0:T(8,128)(2,1)}, u32[]{:S(2)}) copy-start(bf16[6,16,6,16]{3,2,1,0:T(8,128)(2,1)} %get-tuple-element.45) | copy-start | bytes 55300
  49.4 4.6 %copy-start.12 = (bf16[6,16,6,16]{3,2,1,0:T(8,128)(2,1)S(1)}, bf16[6,16,6,16]{3,2,1,0:T(8,128)(2,1)}, u32[]{:S(2)}) copy-start(bf16[6,16,6,16]{3,2,1,0:T(8,128)(2,1)} %get-tuple-element.55) | copy-start | bytes 55300
  49.4 4.6 %copy-start.13 = (bf16[6,16,6,16]{3,2,1,0:T(8,128)(2,1)S(1)}, bf16[6,16,6,16]{3,2,1,0:T(8,128)(2,1)}, u32[]{:S(2)}) copy-start(bf16[6,16,6,16]{3,2,1,0:T(8,128)(2,1)} %get-tuple-element.62) | copy-start | bytes 55300
  50.2 4.3 %copy-start.14 = (bf16[6,16,6,48]{3,2,1,0:T(8,128)(2,1)S(1)}, bf16[6,16,6,48]{3,2,1,0:T(8,128)(2,1)}, u32[]{:S(2)}) copy-start(bf16[6,16,6,48]{3,2,1,0:T(8,128)(2,1)} %get-tuple-element.94) | copy-start | bytes 165892
  50.2 4.4 %copy-start.10 = (bf16[6,16,6,16]{3,2,1,0:T(8,128)(2,1)S(1)}, bf16[6,16,6,16]{3,2,1,0:T(8,128)(2,1)}, u32[]{:S(2)}) copy-start(bf16[6,16,6,16]{3,2,1,0:T(8,128)(2,1)} %get-tuple-element.61) | copy-start | bytes 55300
  54.3 1.0 copy-start.15
  54.3 1.0 copy-start.20
  58.1 3.7 %copy-start.32 = (pred[6,6]{1,0:T(8,128)(4,1)S(1)}, pred[6,6]{1,0:T(8,128)(4,1)}, u32[]{:S(2)}) copy-start(pred[6,6]{1,0:T(8,128)(4,1)} %broadcast_and_fusion) | copy-start | bytes 112
  58.1 3.7 %copy-start.33 = (f32[512]{0:T(512)S(1)}, f32[512]{0:T(512)}, u32[]{:S(2)}) copy-start(f32[512]{0:T(512)} %param.25) | copy-start | bytes 6148
  64.3 2.3 %copy-start.8 = (bf16[4,16,4,512]{3,2,1,0:T(4,128)(2,1)S(1)}, bf16[4,16,4,512]{3,2,1,0:T(4,128)(2,1)}, u32[]{:S(2)}) copy-start(bf16[4,16,4,512]{3,2,1,0:T(4,128)(2,1)} %get-tuple-element.44) | copy-start | bytes 786436
  72.4 2.5 %copy-start.7 = (bf16[4,16,4,512]{3,2,1,0:T(4,128)(2,1)S(1)}, bf16[4,16,4,512]{3,2,1,0:T(4,128)(2,1)}, u32[]{:S(2)}) copy-start(bf16[4,16,4,512]{3,2,1,0:T(4,128)(2,1)} %get-tuple-element.18) | copy-start | bytes 786436
  144.4 1.1 copy-start.1
  145.2 1.2 copy-start.2
  146.0 1.2 copy-start.4
  146.8 1.2 copy-start.5
  147.5 1.2 copy-start.6
  148.3 1.2 copy-start.3
  149.1 1.0 copy-start.9
  149.1 1.0 copy-start.35
  (12 other events, 9.8 us)
Sparse Core Ops, SparseCore 0:
  8.9 131.6 all-gather.1
where the time goes:
time: 159 us; the launch traced here: 158 us
  waiting for transfers between devices  70.6 us (44%)
  local copies, waits for them, and re-layouts  30.1 us (19%)
  other arithmetic  16.3 us (10%)
  between operations  14.7 us (9%)
  starting transfers between devices  12 us (8%)
  blocking collectives  8.74 us (5%)
  matrix products  5.53 us (3%)
    all_gather x1, waiting for transfers between devices, shards(): full_weight = lax.all_gather(conv_weight, 'section', axis=1, tiled=True)  55.2 us
    concatenate x14, other arithmetic, conv_taps(): jnp.concatenate([slab[:, :, 0:columns], slab[:, :, 1:columns + 1], slab[:...  14.1 us
    reshape x18, local copies, waits for them, and re-layouts, conv_taps(): window.reshape(-1, 3 * channels)  10.7 us
    all_to_all x1, waiting for transfers between devices, shards(): lax.all_to_all(outgoing, 'section', split_axis=1, concat_axis=0, tiled=True)  7.51 us
    all_to_all x1, starting transfers between devices, shards(): lax.all_to_all(outgoing, 'section', split_axis=1, concat_axis=0, tiled=True)  6.02 us
    dot_general x18, matrix products, conv_taps(): jnp.dot(window.reshape(-1, 3 * channels), taps, preferred_element_type=jn...  5.17 us
    slice x4, local copies, waits for them, and re-layouts, conv_taps(): slab[:, :, 0:columns]  4.94 us
    slice x2, local copies, waits for them, and re-layouts, conv_taps(): taps = weight[first:first + 3].reshape(3 * channels, weight.shape[2])  4.44 us
  transfers between devices with their start and end apart: 5, of which 5 were waited for; matrix products, arithmetic and copies ran while one was open for 26% of the time, Pallas kernels for 0%

commit v1 on v0

--- a/solution.py
+++ b/solution.py
@@ -1,6 +1,10 @@
+import functools
+
 import jax
 import jax.numpy as jnp
 from jax import lax
+from jax.experimental import pallas as pl
+from jax.experimental.pallas import tpu as pltpu
 from jax.sharding import PartitionSpec as P
 
 D = 6144
@@ -122,6 +126,388 @@
     return decoded.reshape(frames, height, columns, half_channels)
 
 
+def iota(shape, dim):
+    return lax.broadcasted_iota(jnp.int32, shape, dim)
+
+
+def dot(left, right):
+    return jnp.dot(left, right, preferred_element_type=jnp.float32)
+
+
+def pieces(value):
+    high = value.astype(jnp.bfloat16)
+    rest = value - high.astype(jnp.float32)
+    middle = rest.astype(jnp.bfloat16)
+    low = (rest - middle.astype(jnp.float32)).astype(jnp.bfloat16)
+    return high.astype(jnp.float32), middle.astype(jnp.float32), low.astype(jnp.float32)
+
+
+def block_kernel(
+    sizes,
+    hidden,
+    terms,
+    head_weight,
+    head_bias,
+    noisy,
+    step_size,
+    latent_affine,
+    in_weight,
+    in_bias,
+    norm_gain,
+    conv_bias,
+    conv_weight,
+    out,
+    part_a,
+    part_s,
+    part_w,
+    peer_a,
+    peer_s,
+    peer_w,
+    peer_weight,
+    peer_bias,
+    fields,
+    noises,
+    expanded,
+    stacked,
+    taps_in,
+    ups,
+    wide,
+    weight,
+    send_buf,
+    recv_buf,
+    weight_sem,
+    pair_send,
+    pair_recv,
+    noise_send,
+    noise_recv,
+    field_send,
+    field_recv,
+    sum_send,
+    sum_recv,
+):
+    sections, clips_sp, frames, height, columns, lat, channels = sizes
+    rows_i, cols_j = height // 2, columns * sections // 2
+    width = columns * sections
+    tokens = rows_i * cols_j
+    near = frames + 2
+    half = in_weight.shape[2]
+    sec, core, spi = lax.axis_index("section"), lax.axis_index("tp"), lax.axis_index("sp")
+    nxt, prv = lax.rem(spi + 1, clips_sp), lax.rem(spi + clips_sp - 1, clips_sp)
+    peer = {"tp": 1 - core}
+
+    load = pltpu.make_async_copy(conv_weight, weight, weight_sem)
+    load.start()
+    barrier = pltpu.get_barrier_semaphore()
+    pl.semaphore_signal(barrier, inc=1, device_id=peer)
+    for k in range(1, sections):
+        pl.semaphore_signal(barrier, inc=1, device_id={"section": lax.rem(sec + k, sections)})
+    for k in range(sections):
+        pl.semaphore_signal(
+            barrier, inc=1, device_id={"section": lax.rem(sec + k, sections), "sp": prv}
+        )
+    pl.semaphore_wait(barrier, 2 * sections)
+
+    def pair_copy(n, source, target):
+        return pltpu.make_async_remote_copy(
+            source, target, pair_send.at[n], pair_recv.at[n], device_id=peer
+        )
+
+    def spread(source, target, send, recv):
+        made = []
+        for k in range(1, sections):
+            made.append(
+                pltpu.make_async_remote_copy(
+                    source, target.at[0, k], send.at[0, k], recv.at[0, k],
+                    device_id={"section": lax.rem(sec + k, sections)},
+                )
+            )
+        for k in range(sections):
+            made.append(
+                pltpu.make_async_remote_copy(
+                    source, target.at[1, k], send.at[1, k], recv.at[1, k],
+                    device_id={"section": lax.rem(sec + k, sections), "sp": nxt},
+                )
+            )
+        return made
+
+    early = [pair_copy(0, in_weight, peer_weight), pair_copy(1, in_bias, peer_bias)]
+    noise_copies = spread(noisy, noises, noise_send, noise_recv)
+    for c in early + noise_copies:
+        c.start()
+
+    features = hidden.shape[1]
+    values = hidden[...].astype(jnp.float32)
+    own_sum = jnp.sum(values, axis=1, keepdims=True)
+    own_square = jnp.sum(values * values, axis=1, keepdims=True)
+    center = own_sum / features
+    scale, shift = terms[0:1, :], terms[1:2, :]
+    centred = ((values - center) * scale).astype(jnp.bfloat16)
+    part_a[...] = dot(centred, head_weight[...])
+    part_s[...] = jnp.where(iota(part_s.shape, 1) < part_s.shape[1] // 2, own_sum, own_square)
+    row = iota((8, features), 0)
+    lines = jnp.zeros((8, features), jnp.float32)
+    for n, piece in enumerate(pieces(scale) + pieces(shift)):
+        lines = jnp.where(row == n, piece, lines)
+    made = dot(lines.astype(jnp.bfloat16), head_weight[...])
+    line = iota(made.shape, 0)
+    own_scale = jnp.sum(jnp.where(line < 3, made, 0.0), axis=0, keepdims=True)
+    own_shift = jnp.sum(jnp.where(line >= 3, made, 0.0), axis=0, keepdims=True)
+    part_w[...] = jnp.where(line == 0, own_scale, own_shift)
+    pair = [
+        pair_copy(2, part_a, peer_a), pair_copy(3, part_s, peer_s), pair_copy(4, part_w, peer_w)
+    ]
+    for c in pair:
+        c.start()
+    for c in pair:
+        c.wait()
+    far_sum = peer_s[:, 0:1]
+    far_square = peer_s[:, part_s.shape[1] // 2 : part_s.shape[1] // 2 + 1]
+    average = (own_sum + far_sum) / D
+    variance = (own_square + far_square) / D - average * average
+    body = (
+        part_a[...]
+        + peer_a[...]
+        - (average - center) * own_scale
+        - (average - far_sum / features) * peer_w[0:1, :]
+    )
+    velocity = (
+        lax.rsqrt(variance + 1e-06) * body + (own_shift + peer_w[1:2, :]) + head_bias[...]
+    ).astype(jnp.bfloat16)
+    to, at = iota((tokens, tokens), 0), iota((tokens, tokens), 1)
+    swap = (lax.rem(to, rows_i) * cols_j + lax.div(to, rows_i) == at).astype(jnp.bfloat16)
+    fields[0, 0] = dot(swap, velocity).astype(jnp.bfloat16)
+    noises[0, 0] = noisy[...]
+    field_copies = spread(fields.at[0, 0], fields, field_send, field_recv)
+    for c in field_copies:
+        c.start()
+
+    for c in early:
+        c.wait()
+    taps_in[...] = jnp.zeros_like(taps_in)
+    line_size = 4 * 2 * lat
+    for q in range(2):
+        for e in range(3):
+            col = q + e
+            step_j, odd = (col + 1) // 2 - q, (col + 1) % 2
+            for a in range(3):
+                for b in range(3):
+                    tap = 9 * a + 3 * b + e
+                    for p in range(2):
+                        first = step_j * 3 * line_size + a * line_size + (p + b) * 2 * lat + odd * lat
+                        left = p * 2 * half
+                        taps_in[q, first : first + lat, left : left + half] = in_weight[tap]
+                        taps_in[q, first : first + lat, left + half : left + 2 * half] = peer_weight[tap]
+    expanded[...] = jnp.zeros_like(expanded)
+    wide[0] = jnp.zeros_like(wide[0])
+    wide[width + 1] = jnp.zeros_like(wide[0])
+    for c in noise_copies + field_copies:
+        c.wait()
+
+    lanes = 4 * lat
+    src, dst = iota((lanes, line_size), 0), iota((lanes, line_size), 1)
+    place_mid = (src + 2 * lat == dst).astype(jnp.bfloat16)
+    place_before = ((src == dst + 2 * lat) & (dst < 2 * lat)).astype(jnp.bfloat16)
+    place_after = ((src + 6 * lat == dst) & (dst >= 6 * lat)).astype(jnp.bfloat16)
+    i_row = lax.rem(iota((tokens, lanes), 0), rows_i)
+    step = step_size[0]
+    pairs_j = cols_j // sections
+    for slot in range(2):
+        alive = jnp.float32(1.0) if slot == 0 else (spi > 0).astype(jnp.float32)
+        noise_parts = []
+        for g in range(sections):
+            k = lax.rem(sec + sections - g, sections)
+            noise_parts.append(
+                noises[slot, k].astype(jnp.float32).reshape(pairs_j, frames, rows_i, lanes)
+            )
+        for f in range(frames):
+            k = lax.rem(sec + sections - f, sections)
+            field = fields[slot, k].astype(jnp.float32)
+            noise = jnp.concatenate([part[:, f] for part in noise_parts], axis=0)
+            noise = noise.reshape(tokens, lanes)
+            latent = (noise - step * field) * latent_affine[0:1, :] + latent_affine[1:2, :]
+            latent = (latent * alive).astype(jnp.bfloat16).astype(jnp.float32)
+            before = jnp.where(i_row == 0, 0.0, pltpu.roll(latent, 1, 0))
+            after = jnp.where(i_row == rows_i - 1, 0.0, pltpu.roll(latent, tokens - 1, 0))
+            line_values = (
+                dot(before.astype(jnp.bfloat16), place_before)
+                + dot(latent.astype(jnp.bfloat16), place_mid)
+                + dot(after.astype(jnp.bfloat16), place_after)
+            )
+            expanded[1 : cols_j + 1, f + (1 - slot) * frames] = line_values.reshape(
+                cols_j, rows_i, line_size
+            )
+    block = near * rows_i
+    for j in range(cols_j + 2):
+        for a in range(3):
+            stacked[j * block : (j + 1) * block, a * line_size : (a + 1) * line_size] = (
+                expanded[j, a : a + near].reshape(block, line_size).astype(jnp.bfloat16)
+            )
+    parts = half // channels
+    tall = near * height
+    for q in range(2):
+        lhs = jnp.concatenate(
+            [
+                stacked[q * block : (q + cols_j) * block, :],
+                stacked[(q + 1) * block : (q + 1 + cols_j) * block, :],
+            ],
+            axis=1,
+        )
+        for p in range(2):
+            for h in range(2):
+                left = (p * 2 + h) * half
+                bias = in_bias[...] if h == 0 else peer_bias[...]
+                up = dot(lhs, taps_in[q, :, left : left + half]) + bias
+                up = up.astype(jnp.bfloat16).astype(jnp.float32)
+                for j in range(cols_j):
+                    for n in range(parts):
+                        ups[
+                            h * parts + n, pl.ds((2 * j + q) * tall + p, block, stride=2), :
+                        ] = up[j * block : (j + 1) * block, n * channels : (n + 1) * channels]
+
+    mine = lax.rem(sec + parts * core, 2 * parts)
+    gain = norm_gain[pl.ds(sec, 1), :]
+    h_row = lax.rem(iota((tall, channels), 0), height)
+    valid = (spi > 0) | (iota((tall, channels), 0) >= 2 * height)
+
+    def normalise(w, carry):
+        at_w = pl.ds(pl.multiple_of(w * tall, tall), tall)
+        squares = jnp.zeros((tall, channels), jnp.float32)
+        for n in range(2 * parts):
+            g = ups[n, at_w, :]
+            squares = squares + g * g
+        mean = jnp.sum(squares, axis=1, keepdims=True) / (2 * half)
+        v = ups[mine, at_w, :] * lax.rsqrt(mean + 1e-06) * gain
+        v = jnp.where(valid, v / (1.0 + jnp.exp(-v)), 0.0)
+        above = jnp.where(h_row == 0, 0.0, pltpu.roll(v, 1, 0))
+        below = jnp.where(h_row == height - 1, 0.0, pltpu.roll(v, tall - 1, 0))
+        for b, line_v in enumerate((above, v, below)):
+            wide[w + 1, :, b * channels : (b + 1) * channels] = line_v.astype(jnp.bfloat16)
+        return carry
+
+    lax.fori_loop(0, width, normalise, 0)
+    load.wait()
+
+    span = frames * height
+
+    def partial(d):
+        total = jnp.zeros((columns * span, weight.shape[2]), jnp.float32)
+        for a in range(3):
+            for e in range(3):
+                window = wide[pl.ds(d * columns + e, columns), a * height : a * height + span, :]
+                taps = jnp.concatenate([weight[9 * a + 3 * b + e] for b in range(3)], axis=0)
+                total = total + dot(window.reshape(columns * span, 3 * channels), taps)
+        return total
+
+    sums = []
+    for k in range(1, sections):
+        d = lax.rem(sec + k, sections)
+        send_buf[k] = partial(d).astype(jnp.bfloat16)
+        c = pltpu.make_async_remote_copy(
+            send_buf.at[k], recv_buf.at[k], sum_send.at[k], sum_recv.at[k],
+            device_id={"section": d},
+        )
+        c.start()
+        sums.append(c)
+    total = partial(sec) + conv_bias[...]
+    total = total.reshape(columns, span, half)
+    own_w = []
+    for w in range(columns):
+        first = pl.multiple_of((sec * columns + w) * tall + 2 * height, height)
+        own_w.append(
+            jnp.concatenate([ups[n, pl.ds(first, span), :] for n in range(parts)], axis=1)
+        )
+    total = total + jnp.stack(own_w)
+    for c in sums:
+        c.wait()
+    for k in range(1, sections):
+        total = total + recv_buf[k].astype(jnp.float32).reshape(columns, span, half)
+    out[...] = total.astype(out.dtype)
+
+
+def fused_shards(sizes, *arrays):
+    (
+        hidden, modulation, time_embed, head_weight, head_bias, noisy, step_size, latent_mean,
+        latent_std, in_weight, in_bias, norm_gain, conv_weight, conv_bias,
+    ) = arrays
+    sections, clips_sp, frames, height, columns, lat, channels = sizes
+    rows_i, cols_j, half = height // 2, columns * sections // 2, in_weight.shape[2]
+    width, near, tokens, lanes = columns * sections, frames + 2, hidden.shape[0], 4 * lat
+    terms = jnp.stack([1.0 + (modulation[1] + time_embed), modulation[0] + time_embed])
+    noise = noisy.reshape(frames, rows_i, 2, columns // 2, 2, lat)
+    noise = jnp.transpose(noise, (3, 0, 1, 2, 4, 5)).reshape(-1, lanes)
+    affine = jnp.stack([jnp.tile(latent_std, 4), jnp.tile(latent_mean, 4)])
+    line_size = 8 * lat
+    f32, bf16 = jnp.float32, jnp.bfloat16
+    vmem, dma = pltpu.VMEM, pltpu.SemaphoreType.DMA
+    in_vmem = pl.BlockSpec(memory_space=pltpu.VMEM)
+    rows = columns * frames * height
+    out = pl.pallas_call(
+        functools.partial(block_kernel, sizes),
+        out_shape=jax.ShapeDtypeStruct((columns, frames * height, half), bf16),
+        in_specs=[in_vmem] * 5
+        + [pl.BlockSpec(memory_space=pltpu.SMEM)]
+        + [in_vmem] * 5
+        + [pl.BlockSpec(memory_space=pl.ANY)],
+        out_specs=in_vmem,
+        scratch_shapes=[
+            vmem((tokens, lanes), f32),
+            vmem((tokens, 128), f32),
+            vmem((8, lanes), f32),
+            vmem((tokens, lanes), f32),
+            vmem((tokens, 128), f32),
+            vmem((8, lanes), f32),
+            vmem(in_weight.shape, bf16),
+            vmem((1, half), f32),
+            vmem((2, sections, tokens, lanes), bf16),
+            vmem((2, sections, tokens, lanes), bf16),
+            vmem((cols_j + 2, 2 * frames, rows_i, line_size), f32),
+            vmem(((cols_j + 2) * near * rows_i, 3 * line_size), bf16),
+            vmem((2, 6 * line_size, 4 * half), bf16),
+            vmem((2 * half // channels, width * near * height, channels), f32),
+            vmem((width + 2, near * height, 3 * channels), bf16),
+            vmem(conv_weight.shape, bf16),
+            vmem((sections, rows, half), bf16),
+            vmem((sections, rows, half), bf16),
+            dma,
+            dma((5,)),
+            dma((5,)),
+            dma((2, sections)),
+            dma((2, sections)),
+            dma((2, sections)),
+            dma((2, sections)),
+            dma((sections,)),
+            dma((sections,)),
+        ],
+        compiler_params=pltpu.CompilerParams(collective_id=0, has_side_effects=True),
+    )(
+        hidden, terms, head_weight, head_bias[None], noise, step_size, affine, in_weight,
+        in_bias[None], norm_gain.reshape(-1, channels), conv_bias[None], conv_weight,
+    )
+    out = out.reshape(columns, frames, height, half)
+    return jnp.transpose(out, (1, 2, 0, 3))
+
+
+def dispatch(*arrays):
+    hidden, noisy, in_weight, conv_weight = arrays[0], arrays[5], arrays[9], arrays[12]
+    frames, height, columns, lat = noisy.shape
+    sections, cores, clips_sp = (lax.axis_size(axis) for axis in ("section", "tp", "sp"))
+    channels, half = conv_weight.shape[1:]
+    whole_frame = hidden.shape[0] == height // 2 * (columns * sections // 2)
+    if (
+        whole_frame
+        and cores == 2
+        and clips_sp > 1
+        and frames == sections
+        and channels % 128 == 0
+        and half % channels == 0
+        and lat == 16
+        and height == 16
+    ):
+        sizes = (sections, clips_sp, frames, height, columns, lat, channels)
+        return fused_shards(sizes, *arrays)
+    return shards(*arrays)
+
+
 def solution(mesh):
     placed = (
         P(("groups", "sp", "section"), "tp"),
@@ -140,7 +526,7 @@
         P("tp"),
     )
     return jax.shard_map(
-        shards,
+        dispatch,
         mesh=mesh,
         in_specs=placed,
         out_specs=P(("groups", "sp"), None, "section", "tp"),

time: 159 us -> 42.7 us (0.27)
  waiting for transfers between devices: 70.6 us -> 0 us
  Pallas kernels: 0 us -> 31.9 us
  local copies, waits for them, and re-layouts: 30.1 us -> 7.72 us
  other arithmetic: 16.3 us -> 1.9 us
  between operations: 14.7 us -> 0.67 us
  starting transfers between devices: 12 us -> 0 us
  blocking collectives: 8.74 us -> 0 us
  matrix products: 5.53 us -> 0 us
    all_gather x1 -> x0, waiting for transfers between devices: 55.2 us -> none  [shards(): full_weight = lax.all_gather(conv_weight, 'section', axis=1, tiled=True)]
    pallas_call x0 -> x1, Pallas kernels: none -> 31.9 us  [fused_shards(): pl.pallas_call(functools.partial(block_kernel, sizes), out_shape=jax.Shap...]
    concatenate x16 -> x0, other arithmetic: 14.4 us -> none  [the longest x14 14.1 us: conv_taps(): jnp.concatenate([slab[:, :, 0:columns], slab[:, :, 1:columns + 1], slab[:...]
    slice x10 -> x1, local copies, waits for them, and re-layouts: 13.2 us -> 0.83 us  [fused_shards(): modulation[1] + time_embed]
    reshape x23 -> x3, local copies, waits for them, and re-layouts: 13 us -> 3.25 us  [the longest x1 1.66 us: fused_shards(): out = out.reshape(columns, frames, height, half)]
    all_to_all x1 -> x0, waiting for transfers between devices: 7.51 us -> none  [shards(): lax.all_to_all(outgoing, 'section', split_axis=1, concat_axis=0, tiled=True)]
    ppermute x3 -> x0, waiting for transfers between devices: 7.2 us -> none  [the longest x1 4.4 us: padded_2(): after = lax.ppermute(leading, axis, down)]
    psum x2 -> x0, blocking collectives: 6.21 us -> none  [the longest x1 3.58 us: shards(): velocity = (lax.psum(partial_sum, 'tp') + head_bias).astype(jnp.bfloat16)]
  transfers between devices with their start and end apart: 5 -> 0, of which waited for: 5 -> 0; matrix products, arithmetic and copies ran while one was open for 26% -> 0% of each run, Pallas kernels for 0% -> 0%
where the time goes in v1:
time: 42.7 us; the launch traced here: 42.2 us
  Pallas kernels  31.9 us (75%)
  local copies, waits for them, and re-layouts  7.72 us (18%)
  other arithmetic  1.9 us (4%)
  between operations  0.67 us (2%)
    pallas_call x1, Pallas kernels, fused_shards(): pl.pallas_call(functools.partial(block_kernel, sizes), out_shape=jax.Shap...  31.9 us
    unnamed x1, local copies, waits for them, and re-layouts  2.15 us
    reshape x1, local copies, waits for them, and re-layouts, fused_shards(): out = out.reshape(columns, frames, height, half)  1.66 us
    another operation x4, local copies, waits for them, and re-layouts, fused_shards(): affine = jnp.stack([jnp.tile(latent_std, 4), jnp.tile(latent_mean, 4)])  1.48 us
    reshape x1, local copies, waits for them, and re-layouts, fused_shards(): noise = noisy.reshape(frames, rows_i, 2, columns // 2, 2, lat)  0.89 us

profile of v1, /device:TPU:0, one launch (start us, length us, event | category | flops | bytes accessed | tf_op | source)
XLA Modules:
  0.0 42.2 jit_solution(9267609337745119967)
XLA Ops:
  0.7 0.7 %tile.5 = f32[4,16]{1,0:T(4,128)S(1)} broadcast(f32[16]{0:T(128)} %param.21), dimensions={1} | broadcast | bytes 320 | tf_op jit(solution)/shard_map/tile | solution.py:438
  1.3 0.1 stack_tile.7
  1.4 0.7 %tile.4 = f32[4,16]{1,0:T(4,128)S(1)} broadcast(f32[16]{0:T(128)} %param.22), dimensions={1} | broadcast | bytes 320 | tf_op jit(solution)/shard_map/tile | solution.py:438
  2.1 0.1 stack_tile.6
  2.1 0.6 %pad_maximum_fusion.1.latent_affine = f32[2,64]{1,0:T(2,128)} fusion(f32[1,64]{1,0:T(1,128)S(1)} %stack_tile.7, f32[1,64]{1,0:T(1,128)S(1)} %stack_tile.6), kind=kLoop, calls=%fused_computation.4 | loop fusion | flops 128 | bytes 1024 | tf_op jit(solution)/shard_map/stack | solution.py:438
  2.7 0.8 %fusion = (f32[1,3072]{1,0:T(1,128)S(1)}, f32[1,3072]{1,0:T(1,128)S(1)}) fusion(f32[2,3072]{1,0:T(2,128)} %param.15), kind=kLoop, calls=%fused_computation.5 | loop fusion | bytes 49152 | tf_op jit(solution)/shard_map/slice | solution.py:435
  3.5 0.7 %add_add_fusion = (f32[3072]{0:T(1024)S(1)}, f32[3072]{0:T(1024)S(1)}) fusion(f32[3072]{0:T(1024)S(1)} %bitcast.19, f32[3072]{0:T(1024)} %param.16, f32[3072]{0:T(1024)S(1)} %bitcast.20), kind=kLoop, calls=%fused_computation.3 | loop fusion | flops 9216 | bytes 61440 | tf_op jit(solution)/shard_map/add | solution.py:435
  4.2 0.6 %pad_maximum_fusion.terms = f32[2,3072]{1,0:T(2,128)} fusion(f32[1,3072]{1,0:T(1,128)S(1)} %bitcast.22, f32[1,3072]{1,0:T(1,128)S(1)} %bitcast.21), kind=kLoop, calls=%fused_computation.2 | loop fusion | flops 6144 | bytes 49152 | tf_op jit(solution)/shard_map/stack | solution.py:435
  4.9 0.9 %copy.21 = bf16[4,8,2,2,2,16]{5,4,2,1,0,3:T(2,128)(2,1)S(1)} copy(bf16[4,8,2,2,2,16]{5,4,3,2,1,0:T(2,128)(2,1)} %bitcast.18) | data formatting | bytes 16384 | tf_op jit(solution)/shard_map/reshape | solution.py:436
  5.8 0.7 %reshape.15.noisy = bf16[64,64]{1,0:T(8,128)(2,1)} reshape(bf16[2,4,8,2,2,16]{5,4,3,2,1,0:T(2,128)(2,1)S(1)} %bitcast.17) | data formatting | bytes 16384 | tf_op jit(solution)/shard_map/reshape | solution.py:437
  6.5 2.2 %copy.16.head_weight = bf16[3072,64]{1,0:T(8,128)(2,1)} copy(bf16[3072,64]{0,1:T(8,128)(2,1)} %param.17) | data formatting | bytes 786432 | tf_op args[3]
  8.6 31.9 %shard_map.136 = bf16[4,64,256]{2,1,0:T(8,128)(2,1)} custom-call(bf16[64,3072]{1,0:T(8,128)(2,1)} %hidden.1, f32[2,3072]{1,0:T(2,128)} %pad_maximum_fusion.terms, bf16[3072,64]{1,0:T(8,128)(2,1)} %copy.16.head_weight, f32[1,64]{1,0:T(1,128)} %bitcast.26, bf16[64,64]{1,0:T(8,128)(2,1)} %reshape.15.noisy, f32[1]{0:T(128)S(6)} %copy.22.step_size, ...), custom_call_target="tpu_custom_call" | custom-call | tf_op jit(solution)/shard_map/pallas_call | solution.py:444
  40.5 1.7 %copy.20 = bf16[4,4,16,256]{3,0,2,1:T(4,128)(2,1)} copy(bf16[4,4,16,256]{3,2,1,0:T(8,128)(2,1)} %bitcast.16) | data formatting | bytes 262144 | tf_op jit(solution)/shard_map/reshape | solution.py:486

commit v2 on v1

--- a/solution.py
+++ b/solution.py
@@ -134,6 +134,12 @@
     return jnp.dot(left, right, preferred_element_type=jnp.float32)
 
 
+def dot_rows(left, right):
+    return lax.dot_general(
+        left, right, (((1,), (1,)), ((), ())), preferred_element_type=jnp.float32
+    )
+
+
 def pieces(value):
     high = value.astype(jnp.bfloat16)
     rest = value - high.astype(jnp.float32)
@@ -144,19 +150,24 @@
 
 def block_kernel(
     sizes,
-    hidden,
-    terms,
-    head_weight,
+    modulation,
+    time_embed,
     head_bias,
     noisy,
     step_size,
-    latent_affine,
-    in_weight,
+    latent_std,
+    latent_mean,
     in_bias,
     norm_gain,
     conv_bias,
-    conv_weight,
+    hidden_far,
+    head_far,
+    in_far,
+    conv_far,
     out,
+    hidden,
+    head_weight,
+    in_weight,
     part_a,
     part_s,
     part_w,
@@ -175,7 +186,8 @@
     weight,
     send_buf,
     recv_buf,
-    weight_sem,
+    final,
+    load_sems,
     pair_send,
     pair_recv,
     noise_send,
@@ -195,8 +207,14 @@
     nxt, prv = lax.rem(spi + 1, clips_sp), lax.rem(spi + clips_sp - 1, clips_sp)
     peer = {"tp": 1 - core}
 
-    load = pltpu.make_async_copy(conv_weight, weight, weight_sem)
-    load.start()
+    loads = [
+        pltpu.make_async_copy(source, target, load_sems.at[n])
+        for n, (source, target) in enumerate(
+            ((hidden_far, hidden), (head_far, head_weight), (in_far, in_weight), (conv_far, weight))
+        )
+    ]
+    for c in loads:
+        c.start()
     barrier = pltpu.get_barrier_semaphore()
     pl.semaphore_signal(barrier, inc=1, device_id=peer)
     for k in range(1, sections):
@@ -205,7 +223,6 @@
         pl.semaphore_signal(
             barrier, inc=1, device_id={"section": lax.rem(sec + k, sections), "sp": prv}
         )
-    pl.semaphore_wait(barrier, 2 * sections)
 
     def pair_copy(n, source, target):
         return pltpu.make_async_remote_copy(
@@ -230,25 +247,38 @@
             )
         return made
 
-    early = [pair_copy(0, in_weight, peer_weight), pair_copy(1, in_bias, peer_bias)]
-    noise_copies = spread(noisy, noises, noise_send, noise_recv)
-    for c in early + noise_copies:
-        c.start()
+    lanes = 4 * lat
+    share = frames * rows_i * columns // 2
+    to, at = iota((4 * share, 4 * share), 0), iota((4 * share, 4 * share), 1)
+    cell, token = lax.div(to, share), lax.rem(to, share)
+    jl, line_i = lax.div(token, frames * rows_i), lax.rem(token, frames * rows_i)
+    home = (2 * line_i + lax.div(cell, 2)) * columns + 2 * jl + lax.rem(cell, 2)
+    moved = dot((home == at).astype(jnp.bfloat16), noisy[...]).astype(jnp.bfloat16)
+    src, dst = iota((lat, lanes), 0), iota((lat, lanes), 1)
+    own_noise = jnp.zeros((share, lanes), jnp.float32)
+    for n in range(4):
+        own_noise = own_noise + dot(
+            moved[n * share : (n + 1) * share], (src + n * lat == dst).astype(jnp.bfloat16)
+        )
+    noises[0, 0] = own_noise.astype(jnp.bfloat16)
 
     features = hidden.shape[1]
+    scale = 1.0 + (modulation[1:2, :] + time_embed[...])
+    shift = modulation[0:1, :] + time_embed[...]
+    loads[0].wait()
     values = hidden[...].astype(jnp.float32)
     own_sum = jnp.sum(values, axis=1, keepdims=True)
     own_square = jnp.sum(values * values, axis=1, keepdims=True)
     center = own_sum / features
-    scale, shift = terms[0:1, :], terms[1:2, :]
     centred = ((values - center) * scale).astype(jnp.bfloat16)
-    part_a[...] = dot(centred, head_weight[...])
+    loads[1].wait()
+    part_a[...] = dot_rows(centred, head_weight[...])
     part_s[...] = jnp.where(iota(part_s.shape, 1) < part_s.shape[1] // 2, own_sum, own_square)
     row = iota((8, features), 0)
     lines = jnp.zeros((8, features), jnp.float32)
     for n, piece in enumerate(pieces(scale) + pieces(shift)):
         lines = jnp.where(row == n, piece, lines)
-    made = dot(lines.astype(jnp.bfloat16), head_weight[...])
+    made = dot_rows(lines.astype(jnp.bfloat16), head_weight[...])
     line = iota(made.shape, 0)
     own_scale = jnp.sum(jnp.where(line < 3, made, 0.0), axis=0, keepdims=True)
     own_shift = jnp.sum(jnp.where(line >= 3, made, 0.0), axis=0, keepdims=True)
@@ -256,7 +286,11 @@
     pair = [
         pair_copy(2, part_a, peer_a), pair_copy(3, part_s, peer_s), pair_copy(4, part_w, peer_w)
     ]
-    for c in pair:
+    loads[2].wait()
+    early = [pair_copy(0, in_weight, peer_weight), pair_copy(1, in_bias, peer_bias)]
+    noise_copies = spread(noises.at[0, 0], noises, noise_send, noise_recv)
+    pl.semaphore_wait(barrier, 2 * sections)
+    for c in pair + noise_copies + early:
         c.start()
     for c in pair:
         c.wait()
@@ -276,7 +310,6 @@
     to, at = iota((tokens, tokens), 0), iota((tokens, tokens), 1)
     swap = (lax.rem(to, rows_i) * cols_j + lax.div(to, rows_i) == at).astype(jnp.bfloat16)
     fields[0, 0] = dot(swap, velocity).astype(jnp.bfloat16)
-    noises[0, 0] = noisy[...]
     field_copies = spread(fields.at[0, 0], fields, field_send, field_recv)
     for c in field_copies:
         c.start()
@@ -303,13 +336,14 @@
     for c in noise_copies + field_copies:
         c.wait()
 
-    lanes = 4 * lat
     src, dst = iota((lanes, line_size), 0), iota((lanes, line_size), 1)
     place_mid = (src + 2 * lat == dst).astype(jnp.bfloat16)
     place_before = ((src == dst + 2 * lat) & (dst < 2 * lat)).astype(jnp.bfloat16)
     place_after = ((src + 6 * lat == dst) & (dst >= 6 * lat)).astype(jnp.bfloat16)
     i_row = lax.rem(iota((tokens, lanes), 0), rows_i)
     step = step_size[0]
+    std = jnp.concatenate([latent_std[...]] * 4, axis=1)
+    mean_latent = jnp.concatenate([latent_mean[...]] * 4, axis=1)
     pairs_j = cols_j // sections
     for slot in range(2):
         alive = jnp.float32(1.0) if slot == 0 else (spi > 0).astype(jnp.float32)
@@ -324,7 +358,7 @@
             field = fields[slot, k].astype(jnp.float32)
             noise = jnp.concatenate([part[:, f] for part in noise_parts], axis=0)
             noise = noise.reshape(tokens, lanes)
-            latent = (noise - step * field) * latent_affine[0:1, :] + latent_affine[1:2, :]
+            latent = (noise - step * field) * std + mean_latent
             latent = (latent * alive).astype(jnp.bfloat16).astype(jnp.float32)
             before = jnp.where(i_row == 0, 0.0, pltpu.roll(latent, 1, 0))
             after = jnp.where(i_row == rows_i - 1, 0.0, pltpu.roll(latent, tokens - 1, 0))
@@ -385,7 +419,7 @@
         return carry
 
     lax.fori_loop(0, width, normalise, 0)
-    load.wait()
+    loads[3].wait()
 
     span = frames * height
 
@@ -399,7 +433,7 @@
         return total
 
     sums = []
-    for k in range(1, sections):
+    for k in [*range(sections // 2, sections), *range(1, sections // 2)]:
         d = lax.rem(sec + k, sections)
         send_buf[k] = partial(d).astype(jnp.bfloat16)
         c = pltpu.make_async_remote_copy(
@@ -421,7 +455,13 @@
         c.wait()
     for k in range(1, sections):
         total = total + recv_buf[k].astype(jnp.float32).reshape(columns, span, half)
-    out[...] = total.astype(out.dtype)
+    for w in range(columns):
+        for n in range(parts):
+            final[n, pl.ds(w, span, stride=columns), :] = total[
+                w, :, n * channels : (n + 1) * channels
+            ]
+    for n in range(parts):
+        out[:, n * channels : (n + 1) * channels] = final[n].astype(out.dtype)
 
 
 def fused_shards(sizes, *arrays):
@@ -432,10 +472,6 @@
     sections, clips_sp, frames, height, columns, lat, channels = sizes
     rows_i, cols_j, half = height // 2, columns * sections // 2, in_weight.shape[2]
     width, near, tokens, lanes = columns * sections, frames + 2, hidden.shape[0], 4 * lat
-    terms = jnp.stack([1.0 + (modulation[1] + time_embed), modulation[0] + time_embed])
-    noise = noisy.reshape(frames, rows_i, 2, columns // 2, 2, lat)
-    noise = jnp.transpose(noise, (3, 0, 1, 2, 4, 5)).reshape(-1, lanes)
-    affine = jnp.stack([jnp.tile(latent_std, 4), jnp.tile(latent_mean, 4)])
     line_size = 8 * lat
     f32, bf16 = jnp.float32, jnp.bfloat16
     vmem, dma = pltpu.VMEM, pltpu.SemaphoreType.DMA
@@ -443,13 +479,16 @@
     rows = columns * frames * height
     out = pl.pallas_call(
         functools.partial(block_kernel, sizes),
-        out_shape=jax.ShapeDtypeStruct((columns, frames * height, half), bf16),
-        in_specs=[in_vmem] * 5
+        out_shape=jax.ShapeDtypeStruct((rows, half), bf16),
+        in_specs=[in_vmem] * 4
         + [pl.BlockSpec(memory_space=pltpu.SMEM)]
         + [in_vmem] * 5
-        + [pl.BlockSpec(memory_space=pl.ANY)],
+        + [pl.BlockSpec(memory_space=pl.ANY)] * 4,
         out_specs=in_vmem,
         scratch_shapes=[
+            vmem(hidden.shape, bf16),
+            vmem(head_weight.shape[::-1], bf16),
+            vmem(in_weight.shape, bf16),
             vmem((tokens, lanes), f32),
             vmem((tokens, 128), f32),
             vmem((8, lanes), f32),
@@ -468,7 +507,8 @@
             vmem(conv_weight.shape, bf16),
             vmem((sections, rows, half), bf16),
             vmem((sections, rows, half), bf16),
-            dma,
+            vmem((half // channels, rows, channels), f32),
+            dma((4,)),
             dma((5,)),
             dma((5,)),
             dma((2, sections)),
@@ -480,11 +520,11 @@
         ],
         compiler_params=pltpu.CompilerParams(collective_id=0, has_side_effects=True),
     )(
-        hidden, terms, head_weight, head_bias[None], noise, step_size, affine, in_weight,
-        in_bias[None], norm_gain.reshape(-1, channels), conv_bias[None], conv_weight,
-    )
-    out = out.reshape(columns, frames, height, half)
-    return jnp.transpose(out, (1, 2, 0, 3))
+        modulation, time_embed[None], head_bias[None], noisy.reshape(-1, lat), step_size,
+        latent_std[None], latent_mean[None], in_bias[None], norm_gain.reshape(-1, channels),
+        conv_bias[None], hidden, head_weight.T, in_weight, conv_weight,
+    )
+    return out.reshape(frames, height, columns, half)
 
 
 def dispatch(*arrays):

time: 42.7 us -> 33.7 us (0.79)
  local copies, waits for them, and re-layouts: 7.72 us -> 1.6 us
  other arithmetic: 1.9 us -> 0 us
  Pallas kernels: 31.9 us -> 31.2 us
    unnamed x1 -> x0, local copies, waits for them, and re-layouts: 2.15 us -> none
    reshape x3 -> x1, local copies, waits for them, and re-layouts: 3.25 us -> 1.6 us  [fused_shards(): return out.reshape(frames, height, columns, half)]
    another operation x4 -> x0, local copies, waits for them, and re-layouts: 1.48 us -> none  [fused_shards(): affine = jnp.stack([jnp.tile(latent_std, 4), jnp.tile(latent_mean, 4)])]
    another operation x2 -> x0, other arithmetic: 1.18 us -> none  [the longest x1 0.63 us: fused_shards(): jnp.stack([1.0 + (modulation[1] + time_embed), modulation[0] + time_embed])]
    slice x1 -> x0, local copies, waits for them, and re-layouts: 0.83 us -> none  [fused_shards(): modulation[1] + time_embed]
    add x1 -> x0, other arithmetic: 0.71 us -> none  [fused_shards(): 1.0 + (modulation[1] + time_embed)]
    pallas_call x1, Pallas kernels: 31.9 us -> 31.2 us  [fused_shards(): pl.pallas_call(functools.partial(block_kernel, sizes), out_shape=jax.Shap...]
where the time goes in v2:
time: 33.7 us; the launch traced here: 33.5 us
  Pallas kernels  31.2 us (93%)
  local copies, waits for them, and re-layouts  1.6 us (5%)
  between operations  0.66 us (2%)
    pallas_call x1, Pallas kernels, fused_shards(): pl.pallas_call(functools.partial(block_kernel, sizes), out_shape=jax.Shap...  31.2 us
    reshape x1, local copies, waits for them, and re-layouts, fused_shards(): return out.reshape(frames, height, columns, half)  1.6 us

profile of v2, /device:TPU:0, one launch (start us, length us, event | category | flops | bytes accessed | tf_op | source)
XLA Modules:
  0.0 33.5 jit_solution(15606543166116832967)
XLA Ops:
  0.7 31.2 %shard_map.136 = bf16[256,256]{1,0:T(8,128)(2,1)} custom-call(f32[2,3072]{1,0:T(2,128)} %modulation.1, f32[1,3072]{1,0:T(1,128)} %bitcast.11, f32[1,64]{1,0:T(1,128)} %bitcast.15, bf16[256,16]{1,0:T(8,128)(2,1)} %bitcast.10, f32[1]{0:T(128)S(6)} %copy.15.step_size, f32[1,16]{1,0:T(1,128)} %bitcast.16, f32[1,16]{1,0:T(1,128)} %bitcast.17, f32[1,256]{1,0:T(1,128)} %bitcast.13, ...), custom_call_target="tpu_custom_call" | custom-call | tf_op jit(solution)/shard_map/pallas_call | solution.py:480
  31.9 1.6 %reshape.11 = bf16[4,16,4,256]{3,2,1,0:T(4,128)(2,1)} reshape(bf16[256,256]{1,0:T(8,128)(2,1)} %shard_map.136) | data formatting | bytes 262144 | tf_op jit(solution)/shard_map/reshape | solution.py:527

commit v3 on v2

--- a/solution.py
+++ b/solution.py
@@ -137,6 +137,12 @@
 def dot_rows(left, right):
     return lax.dot_general(
         left, right, (((1,), (1,)), ((), ())), preferred_element_type=jnp.float32
+    )
+
+
+def passing(source, target, send, recv, section):
+    return pltpu.make_async_remote_copy(
+        source, target, send, recv, device_id={"section": section}
     )
 
 
@@ -178,6 +184,7 @@
     peer_bias,
     fields,
     noises,
+    noise_own,
     expanded,
     stacked,
     taps_in,
@@ -186,8 +193,11 @@
     weight,
     send_buf,
     recv_buf,
+    relay,
+    held,
     final,
     load_sems,
+    relay_sem,
     pair_send,
     pair_recv,
     noise_send,
@@ -248,10 +258,12 @@
         return made
 
     lanes = 4 * lat
-    share = frames * rows_i * columns // 2
+    tile = rows_i * columns // 2
+    share = frames * tile
     to, at = iota((4 * share, 4 * share), 0), iota((4 * share, 4 * share), 1)
     cell, token = lax.div(to, share), lax.rem(to, share)
-    jl, line_i = lax.div(token, frames * rows_i), lax.rem(token, frames * rows_i)
+    line_f = lax.div(token, tile)
+    jl, line_i = lax.div(lax.rem(token, tile), rows_i), line_f * rows_i + lax.rem(token, rows_i)
     home = (2 * line_i + lax.div(cell, 2)) * columns + 2 * jl + lax.rem(cell, 2)
     moved = dot((home == at).astype(jnp.bfloat16), noisy[...]).astype(jnp.bfloat16)
     src, dst = iota((lat, lanes), 0), iota((lat, lanes), 1)
@@ -260,7 +272,7 @@
         own_noise = own_noise + dot(
             moved[n * share : (n + 1) * share], (src + n * lat == dst).astype(jnp.bfloat16)
         )
-    noises[0, 0] = own_noise.astype(jnp.bfloat16)
+    noise_own[...] = own_noise.astype(jnp.bfloat16).reshape(noise_own.shape)
 
     features = hidden.shape[1]
     scale = 1.0 + (modulation[1:2, :] + time_embed[...])
@@ -288,7 +300,15 @@
     ]
     loads[2].wait()
     early = [pair_copy(0, in_weight, peer_weight), pair_copy(1, in_bias, peer_bias)]
-    noise_copies = spread(noises.at[0, 0], noises, noise_send, noise_recv)
+    noise_copies = []
+    for k in range(1, sections):
+        d = lax.rem(sec + k, sections)
+        noise_copies.append(
+            pltpu.make_async_remote_copy(
+                noise_own.at[d], noises.at[k], noise_send.at[k], noise_recv.at[k],
+                device_id={"section": d},
+            )
+        )
     pl.semaphore_wait(barrier, 2 * sections)
     for c in pair + noise_copies + early:
         c.start()
@@ -309,7 +329,18 @@
     ).astype(jnp.bfloat16)
     to, at = iota((tokens, tokens), 0), iota((tokens, tokens), 1)
     swap = (lax.rem(to, rows_i) * cols_j + lax.div(to, rows_i) == at).astype(jnp.bfloat16)
-    fields[0, 0] = dot(swap, velocity).astype(jnp.bfloat16)
+    field = dot(swap, velocity)
+    for c in noise_copies:
+        c.wait()
+    noises[0] = noise_own[sec]
+    noise = jnp.concatenate(
+        [noises[lax.rem(sec + sections - g, sections)] for g in range(sections)], axis=0
+    ).astype(jnp.float32)
+    std = jnp.concatenate([latent_std[...]] * 4, axis=1)
+    mean_latent = jnp.concatenate([latent_mean[...]] * 4, axis=1)
+    latent = (noise - step_size[0] * field) * std + mean_latent
+    folded = tokens // 2
+    fields[0, 0] = jnp.concatenate([latent[:folded], latent[folded:]], axis=1).astype(jnp.bfloat16)
     field_copies = spread(fields.at[0, 0], fields, field_send, field_recv)
     for c in field_copies:
         c.start()
@@ -333,43 +364,41 @@
     expanded[...] = jnp.zeros_like(expanded)
     wide[0] = jnp.zeros_like(wide[0])
     wide[width + 1] = jnp.zeros_like(wide[0])
-    for c in noise_copies + field_copies:
+    for c in field_copies:
         c.wait()
 
-    src, dst = iota((lanes, line_size), 0), iota((lanes, line_size), 1)
-    place_mid = (src + 2 * lat == dst).astype(jnp.bfloat16)
-    place_before = ((src == dst + 2 * lat) & (dst < 2 * lat)).astype(jnp.bfloat16)
-    place_after = ((src + 6 * lat == dst) & (dst >= 6 * lat)).astype(jnp.bfloat16)
-    i_row = lax.rem(iota((tokens, lanes), 0), rows_i)
-    step = step_size[0]
-    std = jnp.concatenate([latent_std[...]] * 4, axis=1)
-    mean_latent = jnp.concatenate([latent_mean[...]] * 4, axis=1)
-    pairs_j = cols_j // sections
-    for slot in range(2):
-        alive = jnp.float32(1.0) if slot == 0 else (spi > 0).astype(jnp.float32)
-        noise_parts = []
-        for g in range(sections):
-            k = lax.rem(sec + sections - g, sections)
-            noise_parts.append(
-                noises[slot, k].astype(jnp.float32).reshape(pairs_j, frames, rows_i, lanes)
-            )
-        for f in range(frames):
-            k = lax.rem(sec + sections - f, sections)
-            field = fields[slot, k].astype(jnp.float32)
-            noise = jnp.concatenate([part[:, f] for part in noise_parts], axis=0)
-            noise = noise.reshape(tokens, lanes)
-            latent = (noise - step * field) * std + mean_latent
-            latent = (latent * alive).astype(jnp.bfloat16).astype(jnp.float32)
-            before = jnp.where(i_row == 0, 0.0, pltpu.roll(latent, 1, 0))
-            after = jnp.where(i_row == rows_i - 1, 0.0, pltpu.roll(latent, tokens - 1, 0))
-            line_values = (
-                dot(before.astype(jnp.bfloat16), place_before)
-                + dot(latent.astype(jnp.bfloat16), place_mid)
-                + dot(after.astype(jnp.bfloat16), place_after)
-            )
-            expanded[1 : cols_j + 1, f + (1 - slot) * frames] = line_values.reshape(
-                cols_j, rows_i, line_size
-            )
+    shape = (2 * lanes, 2 * line_size)
+    src, dst = iota(shape, 0), iota(shape, 1)
+    same = lax.div(src, lanes) == lax.div(dst, line_size)
+    src, dst = lax.rem(src, lanes), lax.rem(dst, line_size)
+    place_mid = (same & (src + 2 * lat == dst)).astype(jnp.bfloat16)
+    place_before = (same & (src == dst + 2 * lat) & (dst < 2 * lat)).astype(jnp.bfloat16)
+    place_after = (same & (src + 6 * lat == dst) & (dst >= 6 * lat)).astype(jnp.bfloat16)
+    lines_f = jnp.concatenate(
+        [
+            fields[slot, lax.rem(sec + sections - f, sections)]
+            for slot in (1, 0)
+            for f in range(frames)
+        ],
+        axis=0,
+    ).astype(jnp.float32)
+    count = 2 * frames * folded
+    f_row = iota((count, 2 * lanes), 0)
+    i_row = lax.rem(f_row, rows_i)
+    lines_f = jnp.where((f_row >= frames * folded) | (spi > 0), lines_f, 0.0)
+    before = jnp.where(i_row == 0, 0.0, pltpu.roll(lines_f, 1, 0))
+    after = jnp.where(i_row == rows_i - 1, 0.0, pltpu.roll(lines_f, count - 1, 0))
+    line_values = (
+        dot(before.astype(jnp.bfloat16), place_before)
+        + dot(lines_f.astype(jnp.bfloat16), place_mid)
+        + dot(after.astype(jnp.bfloat16), place_after)
+    )
+    half_j = cols_j // 2
+    for f in range(2 * frames):
+        for side in range(2):
+            expanded[1 + side * half_j : 1 + (side + 1) * half_j, f] = line_values[
+                f * folded : (f + 1) * folded, side * line_size : (side + 1) * line_size
+            ].reshape(half_j, rows_i, line_size)
     block = near * rows_i
     for j in range(cols_j + 2):
         for a in range(3):
@@ -432,16 +461,44 @@
                 total = total + dot(window.reshape(columns * span, 3 * channels), taps)
         return total
 
+    mirrored = sec >= sections // 2
+    line = jnp.where(mirrored, sections - 1 - sec, sec)
+
+    def place(n):
+        return jnp.where(mirrored, sections - 1 - n, n)
+
+    last = sections - 2
     sums = []
-    for k in [*range(sections // 2, sections), *range(1, sections // 2)]:
-        d = lax.rem(sec + k, sections)
-        send_buf[k] = partial(d).astype(jnp.bfloat16)
-        c = pltpu.make_async_remote_copy(
-            send_buf.at[k], recv_buf.at[k], sum_send.at[k], sum_recv.at[k],
+    for n in range(sections - 1):
+        d = place(jnp.where(line == 0, sections - 1 - n, jnp.where(line <= n, n + 1, n)))
+        direct = pltpu.make_async_remote_copy(
+            send_buf.at[n], recv_buf.at[sec], sum_send.at[n], sum_recv.at[sec],
             device_id={"section": d},
         )
-        c.start()
-        sums.append(c)
+        sums.append(direct)
+        if n == last:
+            held[...] = partial(d)
+
+            @pl.when(line == 1)
+            def _():
+                passing(send_buf.at[n], relay, sum_send.at[n], relay_sem, place(2)).wait_recv()
+                held[...] += relay[...].astype(jnp.float32)
+
+            send_buf[n] = held[...].astype(jnp.bfloat16)
+            direct.start()
+        elif n == 0:
+            send_buf[n] = partial(d).astype(jnp.bfloat16)
+
+            @pl.when(line == 0)
+            def _():
+                passing(send_buf.at[n], relay, sum_send.at[n], relay_sem, place(1)).start()
+
+            @pl.when(line != 0)
+            def _():
+                direct.start()
+        else:
+            send_buf[n] = partial(d).astype(jnp.bfloat16)
+            direct.start()
     total = partial(sec) + conv_bias[...]
     total = total.reshape(columns, span, half)
     own_w = []
@@ -452,9 +509,17 @@
         )
     total = total + jnp.stack(own_w)
     for c in sums:
-        c.wait()
-    for k in range(1, sections):
-        total = total + recv_buf[k].astype(jnp.float32).reshape(columns, span, half)
+        c.wait_send()
+    held[...] = total.reshape(held.shape)
+    for g in range(sections):
+        gap = jnp.abs(sec - g)
+
+        @pl.when((gap > 0) & (gap < sections - 1))
+        def _():
+            passing(send_buf.at[0], recv_buf.at[g], sum_send.at[0], sum_recv.at[g], g).wait_recv()
+            held[...] += recv_buf[g].astype(jnp.float32)
+
+    total = held[...].reshape(columns, span, half)
     for w in range(columns):
         for n in range(parts):
             final[n, pl.ds(w, span, stride=columns), :] = total[
@@ -497,8 +562,9 @@
             vmem((8, lanes), f32),
             vmem(in_weight.shape, bf16),
             vmem((1, half), f32),
-            vmem((2, sections, tokens, lanes), bf16),
-            vmem((2, sections, tokens, lanes), bf16),
+            vmem((2, sections, tokens // 2, 2 * lanes), bf16),
+            vmem((sections, tokens // sections, lanes), bf16),
+            vmem((frames, tokens // sections, lanes), bf16),
             vmem((cols_j + 2, 2 * frames, rows_i, line_size), f32),
             vmem(((cols_j + 2) * near * rows_i, 3 * line_size), bf16),
             vmem((2, 6 * line_size, 4 * half), bf16),
@@ -507,12 +573,15 @@
             vmem(conv_weight.shape, bf16),
             vmem((sections, rows, half), bf16),
             vmem((sections, rows, half), bf16),
+            vmem((rows, half), bf16),
+            vmem((rows, half), f32),
             vmem((half // channels, rows, channels), f32),
             dma((4,)),
+            dma,
             dma((5,)),
             dma((5,)),
-            dma((2, sections)),
-            dma((2, sections)),
+            dma((sections,)),
+            dma((sections,)),
             dma((2, sections)),
             dma((2, sections)),
             dma((sections,)),
@@ -538,6 +607,7 @@
         and cores == 2
         and clips_sp > 1
         and frames == sections
+        and sections > 3
         and channels % 128 == 0
         and half % channels == 0
         and lat == 16

time: 33.7 us -> 32.6 us (0.967)
  Pallas kernels: 31.2 us -> 30.1 us
    pallas_call x1, Pallas kernels: 31.2 us -> 30.1 us  [fused_shards(): pl.pallas_call(functools.partial(block_kernel, sizes), out_shape=jax.Shap...]
where the time goes in v3:
time: 32.6 us; the launch traced here: 32.4 us
  Pallas kernels  30.1 us (92%)
  local copies, waits for them, and re-layouts  1.6 us (5%)
  between operations  0.66 us (2%)
    pallas_call x1, Pallas kernels, fused_shards(): pl.pallas_call(functools.partial(block_kernel, sizes), out_shape=jax.Shap...  30.1 us
    reshape x1, local copies, waits for them, and re-layouts, fused_shards(): return out.reshape(frames, height, columns, half)  1.6 us

profile of v3, /device:TPU:0, one launch (start us, length us, event | category | flops | bytes accessed | tf_op | source)
XLA Modules:
  0.0 32.4 jit_solution(6499344930747243873)
XLA Ops:
  0.7 30.1 %shard_map.136 = bf16[256,256]{1,0:T(8,128)(2,1)} custom-call(f32[2,3072]{1,0:T(2,128)} %modulation.1, f32[1,3072]{1,0:T(1,128)} %bitcast.11, f32[1,64]{1,0:T(1,128)} %bitcast.15, bf16[256,16]{1,0:T(8,128)(2,1)} %bitcast.10, f32[1]{0:T(128)S(6)} %copy.15.step_size, f32[1,16]{1,0:T(1,128)} %bitcast.16, f32[1,16]{1,0:T(1,128)} %bitcast.17, f32[1,256]{1,0:T(1,128)} %bitcast.13, ...), custom_call_target="tpu_custom_call" | custom-call | tf_op jit(solution)/shard_map/pallas_call | solution.py:545
  30.8 1.6 %reshape.11 = bf16[4,16,4,256]{3,2,1,0:T(4,128)(2,1)} reshape(bf16[256,256]{1,0:T(8,128)(2,1)} %shard_map.136) | data formatting | bytes 262144 | tf_op jit(solution)/shard_map/reshape | solution.py:596

commit v4 on v3

--- a/solution.py
+++ b/solution.py
@@ -137,12 +137,6 @@
 def dot_rows(left, right):
     return lax.dot_general(
         left, right, (((1,), (1,)), ((), ())), preferred_element_type=jnp.float32
-    )
-
-
-def passing(source, target, send, recv, section):
-    return pltpu.make_async_remote_copy(
-        source, target, send, recv, device_id={"section": section}
     )
 
 
@@ -193,11 +187,8 @@
     weight,
     send_buf,
     recv_buf,
-    relay,
-    held,
     final,
     load_sems,
-    relay_sem,
     pair_send,
     pair_recv,
     noise_send,
@@ -461,44 +452,16 @@
                 total = total + dot(window.reshape(columns * span, 3 * channels), taps)
         return total
 
-    mirrored = sec >= sections // 2
-    line = jnp.where(mirrored, sections - 1 - sec, sec)
-
-    def place(n):
-        return jnp.where(mirrored, sections - 1 - n, n)
-
-    last = sections - 2
     sums = []
-    for n in range(sections - 1):
-        d = place(jnp.where(line == 0, sections - 1 - n, jnp.where(line <= n, n + 1, n)))
-        direct = pltpu.make_async_remote_copy(
-            send_buf.at[n], recv_buf.at[sec], sum_send.at[n], sum_recv.at[sec],
+    for k in [*range(sections // 2, sections), *range(1, sections // 2)]:
+        d = lax.rem(sec + k, sections)
+        send_buf[k] = partial(d).astype(jnp.bfloat16)
+        c = pltpu.make_async_remote_copy(
+            send_buf.at[k], recv_buf.at[k], sum_send.at[k], sum_recv.at[k],
             device_id={"section": d},
         )
-        sums.append(direct)
-        if n == last:
-            held[...] = partial(d)
-
-            @pl.when(line == 1)
-            def _():
-                passing(send_buf.at[n], relay, sum_send.at[n], relay_sem, place(2)).wait_recv()
-                held[...] += relay[...].astype(jnp.float32)
-
-            send_buf[n] = held[...].astype(jnp.bfloat16)
-            direct.start()
-        elif n == 0:
-            send_buf[n] = partial(d).astype(jnp.bfloat16)
-
-            @pl.when(line == 0)
-            def _():
-                passing(send_buf.at[n], relay, sum_send.at[n], relay_sem, place(1)).start()
-
-            @pl.when(line != 0)
-            def _():
-                direct.start()
-        else:
-            send_buf[n] = partial(d).astype(jnp.bfloat16)
-            direct.start()
+        c.start()
+        sums.append(c)
     total = partial(sec) + conv_bias[...]
     total = total.reshape(columns, span, half)
     own_w = []
@@ -509,17 +472,9 @@
         )
     total = total + jnp.stack(own_w)
     for c in sums:
-        c.wait_send()
-    held[...] = total.reshape(held.shape)
-    for g in range(sections):
-        gap = jnp.abs(sec - g)
-
-        @pl.when((gap > 0) & (gap < sections - 1))
-        def _():
-            passing(send_buf.at[0], recv_buf.at[g], sum_send.at[0], sum_recv.at[g], g).wait_recv()
-            held[...] += recv_buf[g].astype(jnp.float32)
-
-    total = held[...].reshape(columns, span, half)
+        c.wait()
+    for k in range(1, sections):
+        total = total + recv_buf[k].astype(jnp.float32).reshape(columns, span, half)
     for w in range(columns):
         for n in range(parts):
             final[n, pl.ds(w, span, stride=columns), :] = total[
@@ -573,11 +528,8 @@
             vmem(conv_weight.shape, bf16),
             vmem((sections, rows, half), bf16),
             vmem((sections, rows, half), bf16),
-            vmem((rows, half), bf16),
-            vmem((rows, half), f32),
             vmem((half // channels, rows, channels), f32),
             dma((4,)),
-            dma,
             dma((5,)),
             dma((5,)),
             dma((sections,)),
@@ -607,7 +559,6 @@
         and cores == 2
         and clips_sp > 1
         and frames == sections
-        and sections > 3
         and channels % 128 == 0
         and half % channels == 0
         and lat == 16

time: 32.6 us -> 32.4 us (level)
  no operation moved by 1% of the time
where the time goes in v4:
time: 32.4 us; the launch traced here: 32.2 us
  Pallas kernels  29.9 us (92%)
  local copies, waits for them, and re-layouts  1.6 us (5%)
  between operations  0.66 us (2%)
    pallas_call x1, Pallas kernels, fused_shards(): pl.pallas_call(functools.partial(block_kernel, sizes), out_shape=jax.Shap...  29.9 us
    reshape x1, local copies, waits for them, and re-layouts, fused_shards(): return out.reshape(frames, height, columns, half)  1.6 us

profile of v4, /device:TPU:0, one launch (start us, length us, event | category | flops | bytes accessed | tf_op | source)
XLA Modules:
  0.0 32.2 jit_solution(7438514607187188730)
XLA Ops:
  0.7 29.9 %shard_map.136 = bf16[256,256]{1,0:T(8,128)(2,1)} custom-call(f32[2,3072]{1,0:T(2,128)} %modulation.1, f32[1,3072]{1,0:T(1,128)} %bitcast.11, f32[1,64]{1,0:T(1,128)} %bitcast.15, bf16[256,16]{1,0:T(8,128)(2,1)} %bitcast.10, f32[1]{0:T(128)S(6)} %copy.15.step_size, f32[1,16]{1,0:T(1,128)} %bitcast.16, f32[1,16]{1,0:T(1,128)} %bitcast.17, f32[1,256]{1,0:T(1,128)} %bitcast.13, ...), custom_call_target="tpu_custom_call" | custom-call | tf_op jit(solution)/shard_map/pallas_call | solution.py:500
  30.6 1.6 %reshape.11 = bf16[4,16,4,256]{3,2,1,0:T(4,128)(2,1)} reshape(bf16[256,256]{1,0:T(8,128)(2,1)} %shard_map.136) | data formatting | bytes 262144 | tf_op jit(solution)/shard_map/reshape | solution.py:548
